TPU v7x, 256 devices: a whole 4x4x8 slice. The times are simulated.
256 devices in a mesh: row: 16 (over x, y), col: 16 (over z, core).
Axes of the slice: x: 4, y: 4, z: 8, core: 2. Of those that a mesh axis runs over, the one named last changes fastest.
Arguments:
- values: bfloat16 [8192, 8192], P('row', 'col'), may hold values from 0.0001296997 to 0.12988281
- tile_mask: int32 [64, 64], P('row', 'col'), may hold values 0 or 1
- keep_mask: int32 [64, 64], P('row', 'col'), may hold values 0 or 1
- thr_index: int32 [8192], P('col'), may hold values from 0 to 9
Outputs:
- expanded: bfloat16 [8192, 8192], P('row', 'col')
All inputs are finite; a program needn't handle non-finite values. No bound on the sum of `tile_mask` or of `keep_mask` on one device may be relied on, other than what follows from the above.
Results may differ from a plain program's by a relative error of at most 0.0004.
Values may be sent and summed in bfloat16 or wider, within the bound.
A program may use at most 64 MiB of HBM per device.

v0:
```python
import jax
import jax.numpy as jnp
from jax import lax
from jax.sharding import Mesh
from jax.sharding import PartitionSpec as P

TB = 128
ROW = ("row_0", "row_1")


def over_axes(x, axes):
    for axis in axes:
        x = lax.psum(x, axis)
    return x


def on_device(values, tile_mask, keep_mask, thr_index):
    row_count, col_count = values.shape
    row_tiles = row_count // TB
    col_tiles = col_count // TB
    matrix = (
        values.reshape(row_tiles, TB, col_tiles, TB)
        * tile_mask[:, None, :, None].astype(jnp.bfloat16)
    ).reshape(row_count, col_count)
    kept_cells = jnp.broadcast_to(
        keep_mask[:, None, :, None].astype(jnp.float32), (row_tiles, TB, col_tiles, TB)
    ).reshape(row_count, col_count)
    order_all = row_count * lax.axis_size(ROW)
    thresholds = 0.125 * thr_index.astype(jnp.float32)
    col_panel = lax.all_gather(matrix, ROW, axis=0, tiled=True)
    product = jnp.dot(
        lax.all_gather(matrix, "col", axis=1, tiled=True),
        col_panel,
        preferred_element_type=jnp.float32,
    )
    outputs = []
    for phase_idx in range(col_tiles):
        lo_col = phase_idx * TB
        part_prod = product[:, lo_col : lo_col + TB]
        col_means = over_axes(jnp.sum(part_prod, axis=0), ROW) / order_all
        pruned = (
            jnp.maximum(part_prod - thresholds[lo_col : lo_col + TB] * col_means, 0.0)
            * kept_cells[:, lo_col : lo_col + TB]
        )
        col_totals = over_axes(jnp.sum(pruned, axis=0), ROW) / order_all
        outputs.append(pruned / jnp.maximum(col_totals, 0.1))
    result = jnp.concatenate(outputs, axis=1)
    return result.astype(jnp.bfloat16)


def solution(mesh):
    finer = Mesh(mesh.devices.reshape(4, 4, mesh.shape["col"]), ("row_0", "row_1", "col"))
    placed = (P(ROW, "col"), P(ROW, "col"), P(ROW, "col"), P("col"))
    return jax.shard_map(
        on_device, mesh=finer, in_specs=placed, out_specs=P(ROW, "col"), check_vma=False
    )
```

profile of v0, /device:TPU:2, one launch (start us, length us, event | category | flops | bytes accessed | tf_op | source)
XLA Modules:
  0.0 198.9 jit_solution(1561034129201004434)
XLA Ops:
  6.5 0.0 all-gather.3.cloned.1.call-start
  6.5 0.7 convert_element_type.12
  7.2 0.2 mul.41
  7.4 1.9 bitcast_multiply_fusion
  9.3 0.0 all-gather.3.cloned.1.call-update
  9.4 0.0 all-gather.5.cloned.1.call-start
  9.4 0.7 all-gather.5.cloned.1.call-update
  10.1 0.7 convert_element_type.14
  10.8 0.2 broadcast_in_dim.2
  11.0 0.1 copy.9
  11.1 0.7 convert_multiply_fusion
  11.8 56.5 %all-gather.3.cloned.1.call-done = bf16[512,8192]{1,0:T(8,128)(2,1)} async-done(((bf16[512,512]{1,0:T(8,128)(2,1)}), bf16[512,8192]{1,0:T(8,128)(2,1)}) %all-gather.3.cloned.1.call-update) | async-done | bytes 8388624 | tf_op jit(solution)/shard_map/all_gather | solution.py:32
  68.3 76.8 %all-gather.5.cloned.1.call-done = bf16[8192,512]{1,0:T(8,128)(2,1)} async-done(((bf16[512,512]{1,0:T(8,128)(2,1)}), bf16[8192,512]{1,0:T(8,128)(2,1)}) %all-gather.5.cloned.1.call-update) | async-done | bytes 8388624 | tf_op jit(solution)/shard_map/all_gather | solution.py:30
  145.1 9.4 %fusion.4 = f32[512,512]{1,0:T(8,128)S(1)} fusion(bf16[512,8192]{1,0:T(8,128)(2,1)} %all-gather.3.cloned.1.call-done, bf16[8192,512]{1,0:T(8,128)(2,1)} %all-gather.5.cloned.1.call-done), kind=kOutput, calls=%fused_computation.28 | convolution fusion | flops 4294967296 | bytes 17825792 | tf_op jit(solution)/shard_map/dot_general | solution.py:31
  154.6 0.1 slice_reduce_fusion.3
  154.7 8.6 %all-reduce.3 = (f32[128]{0:T(128)S(1)}, f32[128]{0:T(128)S(1)}, f32[128]{0:T(128)S(1)}, f32[128]{0:T(128)S(1)}) all-reduce(f32[128]{0:T(128)S(1)} %get-tuple-element.9, f32[128]{0:T(128)S(1)} %get-tuple-element.10, f32[128]{0:T(128)S(1)} %get-tuple-element.11, ...), channel_id=1, replica_groups=mesh['row_0'=4,'row_1'=4,'col'=16] {'row_0'}, use_global_device_ids=true, to_apply=%region_1.0 | all-reduce | flops 512 | bytes 4096 | tf_op jit(solution)/shard_map/psum | solution.py:13
  163.3 10.1 %all-reduce.1 = (f32[128]{0:T(128)S(1)}, f32[128]{0:T(128)S(1)}, f32[128]{0:T(128)S(1)}, f32[128]{0:T(128)S(1)}) all-reduce(f32[128]{0:T(128)S(1)} %get-tuple-element.25, f32[128]{0:T(128)S(1)} %get-tuple-element.26, f32[128]{0:T(128)S(1)} %get-tuple-element.27, ...), channel_id=1, replica_groups=mesh['row_0'=4,'row_1'=4,'col'=16] {'row_1'}, use_global_device_ids=true, to_apply=%region_2.0 | all-reduce | flops 512 | bytes 4096 | tf_op jit(solution)/shard_map/psum | solution.py:13
  173.4 0.2 fusion
  173.5 8.6 %all-reduce.2 = (f32[128]{0:T(128)S(1)}, f32[128]{0:T(128)S(1)}, f32[128]{0:T(128)S(1)}, f32[128]{0:T(128)S(1)}) all-reduce(f32[128]{0:T(128)S(1)} %get-tuple-element.6, f32[128]{0:T(128)S(1)} %get-tuple-element.7, f32[128]{0:T(128)S(1)} %get-tuple-element.8, ...), channel_id=1, replica_groups=mesh['row_0'=4,'row_1'=4,'col'=16] {'row_0'}, use_global_device_ids=true, to_apply=%region_22.0 | all-reduce | flops 512 | bytes 4096 | tf_op jit(solution)/shard_map/psum | solution.py:13
  182.1 8.9 %all-reduce = (f32[128]{0:T(128)S(1)}, f32[128]{0:T(128)S(1)}, f32[128]{0:T(128)S(1)}, f32[128]{0:T(128)S(1)}) all-reduce(f32[128]{0:T(128)S(1)} %get-tuple-element.21, f32[128]{0:T(128)S(1)} %get-tuple-element.22, f32[128]{0:T(128)S(1)} %get-tuple-element.23, ...), channel_id=1, replica_groups=mesh['row_0'=4,'row_1'=4,'col'=16] {'row_1'}, use_global_device_ids=true, to_apply=%region_23.0 | all-reduce | flops 512 | bytes 4096 | tf_op jit(solution)/shard_map/psum | solution.py:13
  191.1 0.2 divide_convert_fusion.3
  191.2 0.9 pad_maximum_fusion
  (3 shorter events, 0.0 us)
Async XLA Ops:
  6.5 61.8 %all-gather.3.cloned.1.call-start = ((), (), s32[]{:S(2)}) async-start(), calls=%async_computation | async-start | bytes 8912896 | tf_op jit(solution)/shard_map/all_gather | solution.py:32
  9.4 135.8 %all-gather.5.cloned.1.call-start = ((), (), s32[]{:S(2)}) async-start(), calls=%async_computation.1 | async-start | bytes 8912896 | tf_op jit(solution)/shard_map/all_gather | solution.py:30
Sparse Core Ops, SparseCore 0:
  9.5 58.7 all-gather.2
  70.7 74.3 all-gather.4
where the time goes:
time: 199 us
  waiting for transfers between devices  134 us (67%)
  blocking collectives  36.2 us (18%)
  between operations  13.4 us (7%)
  matrix products  9.44 us (5%)
  other arithmetic  5.27 us (3%)
    all_gather x1, waiting for transfers between devices, on_device(): col_panel = lax.all_gather(matrix, ROW, axis=0, tiled=True)  76.8 us
    all_gather x1, waiting for transfers between devices, on_device(): lax.all_gather(matrix, 'col', axis=1, tiled=True)  56.5 us
    psum x4, blocking collectives, over_axes(): x = lax.psum(x, axis)  36.2 us
    dot_general x1, matrix products, on_device(): jnp.dot(lax.all_gather(matrix, 'col', axis=1, tiled=True), col_panel, pre...  9.44 us
  transfers between devices with their start and end apart: 2, of which 2 were waited for; matrix products, arithmetic and copies ran while one was open for 1% of the time, Pallas kernels for 0%

commit v1 on v0

--- a/solution.py
+++ b/solution.py
@@ -3,6 +3,7 @@
 from jax import lax
 from jax.sharding import Mesh
 from jax.sharding import PartitionSpec as P
+from jax.lax import axis_index, axis_size, ppermute
 
 TB = 128
 ROW = ("row_0", "row_1")
@@ -28,11 +29,25 @@
     order_all = row_count * lax.axis_size(ROW)
     thresholds = 0.125 * thr_index.astype(jnp.float32)
     col_panel = lax.all_gather(matrix, ROW, axis=0, tiled=True)
-    product = jnp.dot(
-        lax.all_gather(matrix, "col", axis=1, tiled=True),
-        col_panel,
-        preferred_element_type=jnp.float32,
-    )
+
+    def pair_ladders(block_here):
+        across = "col"
+        dev_n = axis_size(across)
+        history = list(map(lambda no: (no, (no + 1) % dev_n), range(dev_n)))
+        rack = list(map(lambda no: (no, (no - 1) % dev_n), range(dev_n)))
+        u_next, ready = ([block_here], [block_here])
+        for _ in range(dev_n // 2):
+            u_next.append(ppermute(u_next[-1], across, history))
+        for _ in tuple(range((dev_n - 1) // 2)):
+            ready.append(ppermute(ready[-1], across, rack))
+        big = jnp.roll(
+            jnp.concatenate([*u_next[::-1], *ready[1:]], axis=1),
+            (axis_index(across) - dev_n // 2) * block_here.shape[1],
+            axis=1,
+        )
+        return big
+
+    product = jnp.dot(pair_ladders(matrix), col_panel, preferred_element_type=jnp.float32)
     outputs = []
     for phase_idx in range(col_tiles):
         lo_col = phase_idx * TB

time: 199 us -> 191 us (0.960)
  waiting for transfers between devices: 134 us -> 55 us
  local copies, waits for them, and re-layouts: 0.48 us -> 46 us
  starting transfers between devices: 0.04 us -> 23.1 us
    all_gather x1, waiting for transfers between devices: 76.8 us -> 0.01 us  [on_device(): col_panel = lax.all_gather(matrix, ROW, axis=0, tiled=True)]
    all_gather x1 -> x0, waiting for transfers between devices: 56.5 us -> none  [on_device(): lax.all_gather(matrix, 'col', axis=1, tiled=True)]
    ppermute x0 -> x15, waiting for transfers between devices: none -> 55 us  [the longest x8 49.2 us: pair_ladders(): u_next.append(ppermute(u_next[-1], across, history))]
    unnamed x1 -> x62, local copies, waits for them, and re-layouts: 0.07 us -> 44.7 us
    ppermute x0 -> x15, starting transfers between devices: none -> 23.1 us  [the longest x7 23 us: pair_ladders(): ready.append(ppermute(ready[-1], across, rack))]
  transfers between devices with their start and end apart: 2 -> 16, of which waited for: 2 -> 14; matrix products, arithmetic and copies ran while one was open for 1% -> 24% of each run, Pallas kernels for 0% -> 0%
where the time goes in v1:
time: 191 us; the launch traced here: 190 us
  waiting for transfers between devices  55 us (29%)
  local copies, waits for them, and re-layouts  46 us (24%)
  blocking collectives  37.2 us (19%)
  starting transfers between devices  23.1 us (12%)
  between operations  13.6 us (7%)
  matrix products  9.33 us (5%)
  other arithmetic  5.41 us (3%)
    ppermute x8, waiting for transfers between devices, pair_ladders(): u_next.append(ppermute(u_next[-1], across, history))  49.2 us
    unnamed x62, local copies, waits for them, and re-layouts  44.7 us
    psum x4, blocking collectives, over_axes(): x = lax.psum(x, axis)  37.2 us
    ppermute x7, starting transfers between devices, pair_ladders(): ready.append(ppermute(ready[-1], across, rack))  23 us
    dot_general x1, matrix products, on_device(): jnp.dot(pair_ladders(matrix), col_panel, preferred_element_type=jnp.float32)  9.33 us
    ppermute x7, waiting for transfers between devices, pair_ladders(): ready.append(ppermute(ready[-1], across, rack))  5.79 us
  transfers between devices with their start and end apart: 16, of which 14 were waited for; matrix products, arithmetic and copies ran while one was open for 24% of the time, Pallas kernels for 0%

profile of v1, /device:TPU:2, one launch (start us, length us, event | category | flops | bytes accessed | tf_op | source)
XLA Modules:
  0.0 189.6 jit_solution(2530109634139548422)
XLA Ops:
  7.4 1.9 %bitcast_multiply_fusion = bf16[512,512]{1,0:T(8,128)(2,1)} fusion(bf16[512,512]{1,0:T(8,128)(2,1)} %param.4, bf16[64,8,4,128]{3,2,1,0:T(4,128)(2,1)S(1)} %bitcast.13), kind=kLoop, calls=%fused_computation.3 | loop fusion | flops 262144 | bytes 1572864 | tf_op jit(solution)/shard_map/mul | solution.py:23
  9.4 12.4 %collective-permute-done = bf16[512,512]{1,0:T(8,128)(2,1)S(1)} collective-permute-done((bf16[512,512]{1,0:T(8,128)(2,1)}, bf16[512,512]{1,0:T(8,128)(2,1)S(1)}, u32[]{:S(2)}, u32[]{:S(2)}) %collective-permute-start) | collective-permute-done | bytes 524320 | tf_op jit(solution)/shard_map/ppermute | solution.py:40
  21.8 3.0 %collective-permute-start.8 = (bf16[512,512]{1,0:T(8,128)(2,1)}, bf16[512,512]{1,0:T(8,128)(2,1)S(1)}, u32[]{:S(2)}, u32[]{:S(2)}) collective-permute-start(bf16[512,512]{1,0:T(8,128)(2,1)} %bitcast_multiply_fusion), channel_id=1, source_target_pairs={{0,15},{1,0},{2,1},{3,2},{4,3},{5,4},{6,5},{7,6},{8,7},{9,8},{10,9... | collective-permute-start | bytes 1572872 | tf_op jit(solution)/shard_map/ppermute | solution.py:42
  24.7 6.9 %collective-permute-done.1 = bf16[512,512]{1,0:T(8,128)(2,1)S(1)} collective-permute-done((bf16[512,512]{1,0:T(8,128)(2,1)S(1)}, bf16[512,512]{1,0:T(8,128)(2,1)S(1)}, u32[]{:S(2)}, u32[]{:S(2)}) %collective-permute-start.1) | collective-permute-done | bytes 524320 | tf_op jit(solution)/shard_map/ppermute | solution.py:40
  31.8 3.4 %collective-permute-start.9 = (bf16[512,512]{1,0:T(8,128)(2,1)S(1)}, bf16[512,512]{1,0:T(8,128)(2,1)S(1)}, u32[]{:S(2)}, u32[]{:S(2)}) collective-permute-start(bf16[512,512]{1,0:T(8,128)(2,1)S(1)} %collective-permute-done.8), channel_id=1, source_target_pairs={{0,15},{1,0},{2,1},{3,2},{4,3},{5,4},{6,5},{7,6},{8,7},{9,8},{10,9... | collective-permute-start | bytes 1572872 | tf_op jit(solution)/shard_map/ppermute | solution.py:42
  35.2 6.2 %collective-permute-done.2 = bf16[512,512]{1,0:T(8,128)(2,1)S(1)} collective-permute-done((bf16[512,512]{1,0:T(8,128)(2,1)S(1)}, bf16[512,512]{1,0:T(8,128)(2,1)S(1)}, u32[]{:S(2)}, u32[]{:S(2)}) %collective-permute-start.2) | collective-permute-done | bytes 524320 | tf_op jit(solution)/shard_map/ppermute | solution.py:40
  41.9 3.1 %collective-permute-start.10 = (bf16[512,512]{1,0:T(8,128)(2,1)S(1)}, bf16[512,512]{1,0:T(8,128)(2,1)S(1)}, u32[]{:S(2)}, u32[]{:S(2)}) collective-permute-start(bf16[512,512]{1,0:T(8,128)(2,1)S(1)} %collective-permute-done.9), channel_id=1, source_target_pairs={{0,15},{1,0},{2,1},{3,2},{4,3},{5,4},{6,5},{7,6},{8,7},{9,8},{10,9... | collective-permute-start | bytes 1572872 | tf_op jit(solution)/shard_map/ppermute | solution.py:42
  45.0 6.2 %collective-permute-done.3 = bf16[512,512]{1,0:T(8,128)(2,1)S(1)} collective-permute-done((bf16[512,512]{1,0:T(8,128)(2,1)S(1)}, bf16[512,512]{1,0:T(8,128)(2,1)S(1)}, u32[]{:S(2)}, u32[]{:S(2)}) %collective-permute-start.3) | collective-permute-done | bytes 524320 | tf_op jit(solution)/shard_map/ppermute | solution.py:40
  52.5 3.1 %collective-permute-start.11 = (bf16[512,512]{1,0:T(8,128)(2,1)S(1)}, bf16[512,512]{1,0:T(8,128)(2,1)S(1)}, u32[]{:S(2)}, u32[]{:S(2)}) collective-permute-start(bf16[512,512]{1,0:T(8,128)(2,1)S(1)} %collective-permute-done.10), channel_id=1, source_target_pairs={{0,15},{1,0},{2,1},{3,2},{4,3},{5,4},{6,5},{7,6},{8,7},{9,8},{10,9... | collective-permute-start | bytes 1572872 | tf_op jit(solution)/shard_map/ppermute | solution.py:42
  55.6 5.5 %collective-permute-done.4 = bf16[512,512]{1,0:T(8,128)(2,1)S(1)} collective-permute-done((bf16[512,512]{1,0:T(8,128)(2,1)S(1)}, bf16[512,512]{1,0:T(8,128)(2,1)S(1)}, u32[]{:S(2)}, u32[]{:S(2)}) %collective-permute-start.4) | collective-permute-done | bytes 524320 | tf_op jit(solution)/shard_map/ppermute | solution.py:40
  63.1 3.5 %collective-permute-start.12 = (bf16[512,512]{1,0:T(8,128)(2,1)S(1)}, bf16[512,512]{1,0:T(8,128)(2,1)}, u32[]{:S(2)}, u32[]{:S(2)}) collective-permute-start(bf16[512,512]{1,0:T(8,128)(2,1)S(1)} %collective-permute-done.11), channel_id=1, source_target_pairs={{0,15},{1,0},{2,1},{3,2},{4,3},{5,4},{6,5},{7,6},{8,7},{9,8},{10,9... | collective-permute-start | bytes 1572872 | tf_op jit(solution)/shard_map/ppermute | solution.py:42
  66.6 4.3 %collective-permute-done.5 = bf16[512,512]{1,0:T(8,128)(2,1)S(1)} collective-permute-done((bf16[512,512]{1,0:T(8,128)(2,1)S(1)}, bf16[512,512]{1,0:T(8,128)(2,1)S(1)}, u32[]{:S(2)}, u32[]{:S(2)}) %collective-permute-start.5) | collective-permute-done | bytes 524320 | tf_op jit(solution)/shard_map/ppermute | solution.py:40
  70.9 2.4 %collective-permute-done.12 = bf16[512,512]{1,0:T(8,128)(2,1)} collective-permute-done((bf16[512,512]{1,0:T(8,128)(2,1)S(1)}, bf16[512,512]{1,0:T(8,128)(2,1)}, u32[]{:S(2)}, u32[]{:S(2)}) %collective-permute-start.12) | collective-permute-done | bytes 524320 | tf_op jit(solution)/shard_map/ppermute | solution.py:42
  73.3 3.5 %collective-permute-start.13 = (bf16[512,512]{1,0:T(8,128)(2,1)}, bf16[512,512]{1,0:T(8,128)(2,1)}, u32[]{:S(2)}, u32[]{:S(2)}) collective-permute-start(bf16[512,512]{1,0:T(8,128)(2,1)} %collective-permute-done.12), channel_id=1, source_target_pairs={{0,15},{1,0},{2,1},{3,2},{4,3},{5,4},{6,5},{7,6},{8,7},{9,8},{10,9... | collective-permute-start | bytes 1572872 | tf_op jit(solution)/shard_map/ppermute | solution.py:42
  76.8 4.0 %collective-permute-done.6 = bf16[512,512]{1,0:T(8,128)(2,1)} collective-permute-done((bf16[512,512]{1,0:T(8,128)(2,1)S(1)}, bf16[512,512]{1,0:T(8,128)(2,1)}, u32[]{:S(2)}, u32[]{:S(2)}) %collective-permute-start.6) | collective-permute-done | bytes 524320 | tf_op jit(solution)/shard_map/ppermute | solution.py:40
  83.8 3.4 %collective-permute-start.14 = (bf16[512,512]{1,0:T(8,128)(2,1)}, bf16[512,512]{1,0:T(8,128)(2,1)S(1)}, u32[]{:S(2)}, u32[]{:S(2)}) collective-permute-start(bf16[512,512]{1,0:T(8,128)(2,1)} %collective-permute-done.13), channel_id=1, source_target_pairs={{0,15},{1,0},{2,1},{3,2},{4,3},{5,4},{6,5},{7,6},{8,7},{9,8},{10,9... | collective-permute-start | bytes 1572872 | tf_op jit(solution)/shard_map/ppermute | solution.py:42
  87.2 3.7 %collective-permute-done.7 = bf16[512,512]{1,0:T(8,128)(2,1)} collective-permute-done((bf16[512,512]{1,0:T(8,128)(2,1)}, bf16[512,512]{1,0:T(8,128)(2,1)}, u32[]{:S(2)}, u32[]{:S(2)}) %collective-permute-start.7) | collective-permute-done | bytes 524320 | tf_op jit(solution)/shard_map/ppermute | solution.py:40
  90.9 1.9 %constant_dynamic-update-slice_fusion.31 = bf16[512,16384]{1,0:T(8,128)(2,1)} fusion(bf16[512,512]{1,0:T(8,128)(2,1)} %collective-permute-done.7), kind=kLoop, calls=%fused_computation.48 | loop fusion | bytes 1048576
  92.8 1.9 %constant_dynamic-update-slice_fusion.30 = bf16[512,16384]{1,0:T(8,128)(2,1)} fusion(bf16[512,16384]{1,0:T(8,128)(2,1)} %constant_dynamic-update-slice_fusion.31, bf16[512,512]{1,0:T(8,128)(2,1)} %collective-permute-done.6), kind=kLoop, calls=%fused_computation.47 | loop fusion | bytes 1048576
  94.7 1.9 %constant_dynamic-update-slice_fusion.29 = bf16[512,16384]{1,0:T(8,128)(2,1)} fusion(bf16[512,16384]{1,0:T(8,128)(2,1)} %constant_dynamic-update-slice_fusion.30, bf16[512,512]{1,0:T(8,128)(2,1)} %copy-done.13), kind=kLoop, calls=%fused_computation.46 | loop fusion | bytes 1048576
  96.6 1.9 %constant_dynamic-update-slice_fusion.28 = bf16[512,16384]{1,0:T(8,128)(2,1)} fusion(bf16[512,16384]{1,0:T(8,128)(2,1)} %constant_dynamic-update-slice_fusion.29, bf16[512,512]{1,0:T(8,128)(2,1)} %copy-done.11), kind=kLoop, calls=%fused_computation.45 | loop fusion | bytes 1048576
  98.6 1.9 %constant_dynamic-update-slice_fusion.27 = bf16[512,16384]{1,0:T(8,128)(2,1)} fusion(bf16[512,16384]{1,0:T(8,128)(2,1)} %constant_dynamic-update-slice_fusion.28, bf16[512,512]{1,0:T(8,128)(2,1)} %copy-done.9), kind=kLoop, calls=%fused_computation.44 | loop fusion | bytes 1048576
  100.5 1.9 constant_dynamic-update-slice_fusion.26
  106.8 1.9 constant_dynamic-update-slice_fusion.21
  110.5 1.9 %constant_dynamic-update-slice_fusion.19 = bf16[512,16384]{1,0:T(8,128)(2,1)} fusion(bf16[512,16384]{1,0:T(8,128)(2,1)} %constant_dynamic-update-slice_fusion.20, bf16[512,512]{1,0:T(8,128)(2,1)} %copy-done.7), kind=kLoop, calls=%fused_computation.36 | loop fusion | bytes 1048576
  117.0 1.9 %constant_dynamic-update-slice_fusion.15 = bf16[512,16384]{1,0:T(8,128)(2,1)} fusion(bf16[512,16384]{1,0:T(8,128)(2,1)} %constant_dynamic-update-slice_fusion.16, bf16[512,512]{1,0:T(8,128)(2,1)} %collective-permute-done.7), kind=kLoop, calls=%fused_computation.32 | loop fusion | bytes 1048576
  132.1 1.9 %constant_dynamic-update-slice_fusion.1 = bf16[512,16384]{1,0:T(8,128)(2,1)} fusion(bf16[512,16384]{1,0:T(8,128)(2,1)} %constant_dynamic-update-slice_fusion.2, bf16[512,512]{1,0:T(8,128)(2,1)} %collective-permute-done.13), kind=kLoop, calls=%fused_computation.18 | loop fusion | bytes 1048576
  134.8 9.3 %fusion = f32[512,512]{1,0:T(8,128)S(1)} fusion(bf16[8192,512]{1,0:T(8,128)(2,1)} %all-gather.2.cloned.1.call-done, bf16[512,16384]{1,0:T(8,128)(2,1)} %constant_dynamic-update-slice_fusion, s32[]{:T(128)S(6)} %select_n.14), kind=kOutput, calls=%fused_computation | convolution fusion | flops 4294967296 | bytes 17825796 | tf_op jit(solution)/shard_map/dot_general | solution.py:50
  144.3 8.6 %all-reduce.3 = (f32[128]{0:T(128)S(1)}, f32[128]{0:T(128)S(1)}, f32[128]{0:T(128)S(1)}, f32[128]{0:T(128)S(1)}) all-reduce(f32[128]{0:T(128)S(1)} %get-tuple-element.9, f32[128]{0:T(128)S(1)} %get-tuple-element.10, f32[128]{0:T(128)S(1)} %get-tuple-element.11, ...), channel_id=1, replica_groups=mesh['row_0'=4,'row_1'=4,'col'=16] {'row_0'}, use_global_device_ids=true, to_apply=%region_1.2 | all-reduce | flops 512 | bytes 4096 | tf_op jit(solution)/shard_map/psum | solution.py:14
  152.9 10.7 %all-reduce.1 = (f32[128]{0:T(128)S(1)}, f32[128]{0:T(128)S(1)}, f32[128]{0:T(128)S(1)}, f32[128]{0:T(128)S(1)}) all-reduce(f32[128]{0:T(128)S(1)} %get-tuple-element.25, f32[128]{0:T(128)S(1)} %get-tuple-element.26, f32[128]{0:T(128)S(1)} %get-tuple-element.27, ...), channel_id=1, replica_groups=mesh['row_0'=4,'row_1'=4,'col'=16] {'row_1'}, use_global_device_ids=true, to_apply=%region_2.3 | all-reduce | flops 512 | bytes 4096 | tf_op jit(solution)/shard_map/psum | solution.py:14
  163.8 10.1 %all-reduce.2 = (f32[128]{0:T(128)S(1)}, f32[128]{0:T(128)S(1)}, f32[128]{0:T(128)S(1)}, f32[128]{0:T(128)S(1)}) all-reduce(f32[128]{0:T(128)S(1)} %get-tuple-element.6, f32[128]{0:T(128)S(1)} %get-tuple-element.7, f32[128]{0:T(128)S(1)} %get-tuple-element.8, ...), channel_id=1, replica_groups=mesh['row_0'=4,'row_1'=4,'col'=16] {'row_0'}, use_global_device_ids=true, to_apply=%region_22.23 | all-reduce | flops 512 | bytes 4096 | tf_op jit(solution)/shard_map/psum | solution.py:14
  173.9 7.7 %all-reduce = (f32[128]{0:T(128)S(1)}, f32[128]{0:T(128)S(1)}, f32[128]{0:T(128)S(1)}, f32[128]{0:T(128)S(1)}) all-reduce(f32[128]{0:T(128)S(1)} %get-tuple-element.21, f32[128]{0:T(128)S(1)} %get-tuple-element.22, f32[128]{0:T(128)S(1)} %get-tuple-element.23, ...), channel_id=1, replica_groups=mesh['row_0'=4,'row_1'=4,'col'=16] {'row_1'}, use_global_device_ids=true, to_apply=%region_23.24 | all-reduce | flops 512 | bytes 4096 | tf_op jit(solution)/shard_map/psum | solution.py:14
  (82 shorter events, 33.9 us)
Async XLA Ops:
  6.5 128.3 %all-gather.2.cloned.1.call-start = ((), (), s32[]{:S(2)}) async-start(), calls=%async_computation | async-start | bytes 8912896 | tf_op jit(solution)/shard_map/all_gather | solution.py:31
  9.3 116.6 %copy-start = (bf16[512,512]{1,0:T(8,128)(2,1)S(1)}, bf16[512,512]{1,0:T(8,128)(2,1)}, u32[]{:S(2)}) copy-start(bf16[512,512]{1,0:T(8,128)(2,1)} %bitcast_multiply_fusion) | copy-start | bytes 1572868
  9.4 12.4 %collective-permute-start = (bf16[512,512]{1,0:T(8,128)(2,1)}, bf16[512,512]{1,0:T(8,128)(2,1)S(1)}, u32[]{:S(2)}, u32[]{:S(2)}) collective-permute-start(bf16[512,512]{1,0:T(8,128)(2,1)} %bitcast_multiply_fusion), channel_id=1, source_target_pairs={{0,1},{1,2},{2,3},{3,4},{4,5},{5,6},{6,7},{7,8},{8,9},{9,10},{10,1... | collective-permute-start | bytes 1572872 | tf_op jit(solution)/shard_map/ppermute | solution.py:40
  21.8 9.8 %collective-permute-start.1 = (bf16[512,512]{1,0:T(8,128)(2,1)S(1)}, bf16[512,512]{1,0:T(8,128)(2,1)S(1)}, u32[]{:S(2)}, u32[]{:S(2)}) collective-permute-start(bf16[512,512]{1,0:T(8,128)(2,1)S(1)} %collective-permute-done), channel_id=1, source_target_pairs={{0,1},{1,2},{2,3},{3,4},{4,5},{5,6},{6,7},{7,8},{8,9},{9,10},{10,1... | collective-permute-start | bytes 1572872 | tf_op jit(solution)/shard_map/ppermute | solution.py:40
  21.8 10.0 %collective-permute-start.8 = (bf16[512,512]{1,0:T(8,128)(2,1)}, bf16[512,512]{1,0:T(8,128)(2,1)S(1)}, u32[]{:S(2)}, u32[]{:S(2)}) collective-permute-start(bf16[512,512]{1,0:T(8,128)(2,1)} %bitcast_multiply_fusion), channel_id=1, source_target_pairs={{0,15},{1,0},{2,1},{3,2},{4,3},{5,4},{6,5},{7,6},{8,7},{9,8},{10,9... | collective-permute-start | bytes 1572872 | tf_op jit(solution)/shard_map/ppermute | solution.py:42
  31.6 9.8 %collective-permute-start.2 = (bf16[512,512]{1,0:T(8,128)(2,1)S(1)}, bf16[512,512]{1,0:T(8,128)(2,1)S(1)}, u32[]{:S(2)}, u32[]{:S(2)}) collective-permute-start(bf16[512,512]{1,0:T(8,128)(2,1)S(1)} %collective-permute-done.1), channel_id=1, source_target_pairs={{0,1},{1,2},{2,3},{3,4},{4,5},{5,6},{6,7},{7,8},{8,9},{9,10},{10,1... | collective-permute-start | bytes 1572872 | tf_op jit(solution)/shard_map/ppermute | solution.py:40
  31.8 10.1 %collective-permute-start.9 = (bf16[512,512]{1,0:T(8,128)(2,1)S(1)}, bf16[512,512]{1,0:T(8,128)(2,1)S(1)}, u32[]{:S(2)}, u32[]{:S(2)}) collective-permute-start(bf16[512,512]{1,0:T(8,128)(2,1)S(1)} %collective-permute-done.8), channel_id=1, source_target_pairs={{0,15},{1,0},{2,1},{3,2},{4,3},{5,4},{6,5},{7,6},{8,7},{9,8},{10,9... | collective-permute-start | bytes 1572872 | tf_op jit(solution)/shard_map/ppermute | solution.py:42
  41.4 40.3 %copy-start.3 = (bf16[512,512]{1,0:T(8,128)(2,1)}, bf16[512,512]{1,0:T(8,128)(2,1)S(1)}, u32[]{:S(2)}) copy-start(bf16[512,512]{1,0:T(8,128)(2,1)S(1)} %collective-permute-done.2) | copy-start | bytes 1572868
  41.4 9.8 %collective-permute-start.3 = (bf16[512,512]{1,0:T(8,128)(2,1)S(1)}, bf16[512,512]{1,0:T(8,128)(2,1)S(1)}, u32[]{:S(2)}, u32[]{:S(2)}) collective-permute-start(bf16[512,512]{1,0:T(8,128)(2,1)S(1)} %collective-permute-done.2), channel_id=1, source_target_pairs={{0,1},{1,2},{2,3},{3,4},{4,5},{5,6},{6,7},{7,8},{8,9},{9,10},{10,1... | collective-permute-start | bytes 1572872 | tf_op jit(solution)/shard_map/ppermute | solution.py:40
  41.9 39.8 %copy-start.1 = (bf16[512,512]{1,0:T(8,128)(2,1)}, bf16[512,512]{1,0:T(8,128)(2,1)S(1)}, u32[]{:S(2)}) copy-start(bf16[512,512]{1,0:T(8,128)(2,1)S(1)} %collective-permute-done.9) | copy-start | bytes 1572868
  41.9 9.8 %collective-permute-start.10 = (bf16[512,512]{1,0:T(8,128)(2,1)S(1)}, bf16[512,512]{1,0:T(8,128)(2,1)S(1)}, u32[]{:S(2)}, u32[]{:S(2)}) collective-permute-start(bf16[512,512]{1,0:T(8,128)(2,1)S(1)} %collective-permute-done.9), channel_id=1, source_target_pairs={{0,15},{1,0},{2,1},{3,2},{4,3},{5,4},{6,5},{7,6},{8,7},{9,8},{10,9... | collective-permute-start | bytes 1572872 | tf_op jit(solution)/shard_map/ppermute | solution.py:42
  51.2 22.1 %copy-start.9 = (bf16[512,512]{1,0:T(8,128)(2,1)}, bf16[512,512]{1,0:T(8,128)(2,1)S(1)}, u32[]{:S(2)}) copy-start(bf16[512,512]{1,0:T(8,128)(2,1)S(1)} %collective-permute-done.3) | copy-start | bytes 1572868
  51.2 9.8 %collective-permute-start.4 = (bf16[512,512]{1,0:T(8,128)(2,1)S(1)}, bf16[512,512]{1,0:T(8,128)(2,1)S(1)}, u32[]{:S(2)}, u32[]{:S(2)}) collective-permute-start(bf16[512,512]{1,0:T(8,128)(2,1)S(1)} %collective-permute-done.3), channel_id=1, source_target_pairs={{0,1},{1,2},{2,3},{3,4},{4,5},{5,6},{6,7},{7,8},{8,9},{9,10},{10,1... | collective-permute-start | bytes 1572872 | tf_op jit(solution)/shard_map/ppermute | solution.py:40
  51.7 0.8 copy-start.5
  52.5 9.8 %collective-permute-start.11 = (bf16[512,512]{1,0:T(8,128)(2,1)S(1)}, bf16[512,512]{1,0:T(8,128)(2,1)S(1)}, u32[]{:S(2)}, u32[]{:S(2)}) collective-permute-start(bf16[512,512]{1,0:T(8,128)(2,1)S(1)} %collective-permute-done.10), channel_id=1, source_target_pairs={{0,15},{1,0},{2,1},{3,2},{4,3},{5,4},{6,5},{7,6},{8,7},{9,8},{10,9... | collective-permute-start | bytes 1572872 | tf_op jit(solution)/shard_map/ppermute | solution.py:42
  61.1 15.8 %copy-start.11 = (bf16[512,512]{1,0:T(8,128)(2,1)}, bf16[512,512]{1,0:T(8,128)(2,1)S(1)}, u32[]{:S(2)}) copy-start(bf16[512,512]{1,0:T(8,128)(2,1)S(1)} %collective-permute-done.4) | copy-start | bytes 1572868
  61.1 9.8 %collective-permute-start.5 = (bf16[512,512]{1,0:T(8,128)(2,1)S(1)}, bf16[512,512]{1,0:T(8,128)(2,1)S(1)}, u32[]{:S(2)}, u32[]{:S(2)}) collective-permute-start(bf16[512,512]{1,0:T(8,128)(2,1)S(1)} %collective-permute-done.4), channel_id=1, source_target_pairs={{0,1},{1,2},{2,3},{3,4},{4,5},{5,6},{6,7},{7,8},{8,9},{9,10},{10,1... | collective-permute-start | bytes 1572872 | tf_op jit(solution)/shard_map/ppermute | solution.py:40
  62.3 0.8 copy-start.7
  63.1 10.2 %collective-permute-start.12 = (bf16[512,512]{1,0:T(8,128)(2,1)S(1)}, bf16[512,512]{1,0:T(8,128)(2,1)}, u32[]{:S(2)}, u32[]{:S(2)}) collective-permute-start(bf16[512,512]{1,0:T(8,128)(2,1)S(1)} %collective-permute-done.11), channel_id=1, source_target_pairs={{0,15},{1,0},{2,1},{3,2},{4,3},{5,4},{6,5},{7,6},{8,7},{9,8},{10,9... | collective-permute-start | bytes 1572872 | tf_op jit(solution)/shard_map/ppermute | solution.py:42
  70.9 9.9 %copy-start.13 = (bf16[512,512]{1,0:T(8,128)(2,1)}, bf16[512,512]{1,0:T(8,128)(2,1)S(1)}, u32[]{:S(2)}) copy-start(bf16[512,512]{1,0:T(8,128)(2,1)S(1)} %collective-permute-done.5) | copy-start | bytes 1572868
  70.9 9.9 %collective-permute-start.6 = (bf16[512,512]{1,0:T(8,128)(2,1)S(1)}, bf16[512,512]{1,0:T(8,128)(2,1)}, u32[]{:S(2)}, u32[]{:S(2)}) collective-permute-start(bf16[512,512]{1,0:T(8,128)(2,1)S(1)} %collective-permute-done.5), channel_id=1, source_target_pairs={{0,1},{1,2},{2,3},{3,4},{4,5},{5,6},{6,7},{7,8},{8,9},{9,10},{10,1... | collective-permute-start | bytes 1572872 | tf_op jit(solution)/shard_map/ppermute | solution.py:40
  73.3 10.5 %collective-permute-start.13 = (bf16[512,512]{1,0:T(8,128)(2,1)}, bf16[512,512]{1,0:T(8,128)(2,1)}, u32[]{:S(2)}, u32[]{:S(2)}) collective-permute-start(bf16[512,512]{1,0:T(8,128)(2,1)} %collective-permute-done.12), channel_id=1, source_target_pairs={{0,15},{1,0},{2,1},{3,2},{4,3},{5,4},{6,5},{7,6},{8,7},{9,8},{10,9... | collective-permute-start | bytes 1572872 | tf_op jit(solution)/shard_map/ppermute | solution.py:42
  80.8 10.1 %collective-permute-start.7 = (bf16[512,512]{1,0:T(8,128)(2,1)}, bf16[512,512]{1,0:T(8,128)(2,1)}, u32[]{:S(2)}, u32[]{:S(2)}) collective-permute-start(bf16[512,512]{1,0:T(8,128)(2,1)} %collective-permute-done.6), channel_id=1, source_target_pairs={{0,1},{1,2},{2,3},{3,4},{4,5},{5,6},{6,7},{7,8},{8,9},{9,10},{10,1... | collective-permute-start | bytes 1572872 | tf_op jit(solution)/shard_map/ppermute | solution.py:40
  81.8 39.0 %copy-start.14 = (bf16[512,512]{1,0:T(8,128)(2,1)S(1)}, bf16[512,512]{1,0:T(8,128)(2,1)}, u32[]{:S(2)}) copy-start(bf16[512,512]{1,0:T(8,128)(2,1)} %copy-done.13) | copy-start | bytes 1572868
  81.8 39.9 %copy-start.12 = (bf16[512,512]{1,0:T(8,128)(2,1)S(1)}, bf16[512,512]{1,0:T(8,128)(2,1)}, u32[]{:S(2)}) copy-start(bf16[512,512]{1,0:T(8,128)(2,1)} %copy-done.11) | copy-start | bytes 1572868
  81.8 40.7 %copy-start.10 = (bf16[512,512]{1,0:T(8,128)(2,1)S(1)}, bf16[512,512]{1,0:T(8,128)(2,1)}, u32[]{:S(2)}) copy-start(bf16[512,512]{1,0:T(8,128)(2,1)} %copy-done.9) | copy-start | bytes 1572868
  81.8 41.6 %copy-start.4 = (bf16[512,512]{1,0:T(8,128)(2,1)S(1)}, bf16[512,512]{1,0:T(8,128)(2,1)}, u32[]{:S(2)}) copy-start(bf16[512,512]{1,0:T(8,128)(2,1)} %copy-done.3) | copy-start | bytes 1572868
  81.8 45.8 %copy-start.2 = (bf16[512,512]{1,0:T(8,128)(2,1)S(1)}, bf16[512,512]{1,0:T(8,128)(2,1)}, u32[]{:S(2)}) copy-start(bf16[512,512]{1,0:T(8,128)(2,1)} %copy-done.1) | copy-start | bytes 1572868
  81.9 46.6 %copy-start.6 = (bf16[512,512]{1,0:T(8,128)(2,1)S(1)}, bf16[512,512]{1,0:T(8,128)(2,1)}, u32[]{:S(2)}) copy-start(bf16[512,512]{1,0:T(8,128)(2,1)} %copy-done.5) | copy-start | bytes 1572868
  81.9 47.5 %copy-start.8 = (bf16[512,512]{1,0:T(8,128)(2,1)S(1)}, bf16[512,512]{1,0:T(8,128)(2,1)}, u32[]{:S(2)}) copy-start(bf16[512,512]{1,0:T(8,128)(2,1)} %copy-done.7) | copy-start | bytes 1572868
  83.8 32.4 %collective-permute-start.14 = (bf16[512,512]{1,0:T(8,128)(2,1)}, bf16[512,512]{1,0:T(8,128)(2,1)S(1)}, u32[]{:S(2)}, u32[]{:S(2)}) collective-permute-start(bf16[512,512]{1,0:T(8,128)(2,1)} %collective-permute-done.13), channel_id=1, source_target_pairs={{0,15},{1,0},{2,1},{3,2},{4,3},{5,4},{6,5},{7,6},{8,7},{9,8},{10,9... | collective-permute-start | bytes 1572872 | tf_op jit(solution)/shard_map/ppermute | solution.py:42
Sparse Core Ops, SparseCore 0:
  9.8 78.7 all-gather.1
